TPU v7x, 32 devices: a whole 2x2x4 slice. The times are simulated.
32 devices in a mesh: lat: 4 (over y, x), lon: 8 (over z, core).
Axes of the slice: x: 2, y: 2, z: 4, core: 2. Of those that a mesh axis runs over, the one named last changes fastest.
Arguments:
- transport: bfloat16 [48, 512, 3072], P(None, 'lat', 'lon'), may hold values from -0.0625 to 0.0625
- sigma_class: int32 [48, 512, 3072], P(None, 'lat', 'lon'), may hold values from 0 to 199
- basin_id: int32 [512, 3072], P('lat', 'lon'), may hold values from 0 to 3
- depth_levels: int32 [512, 3072], P('lat', 'lon'), may hold values from 0 to 48
Outputs:
- overturning: bfloat16 [4, 200, 512], replicated
Inputs may be any that keep to these rules, and one draw needn't show every extreme that they name: `depth_levels`: 0 marks a land column.
All inputs are finite; a program needn't handle non-finite values.
Results may differ from a plain program's by a relative error of at most 0.001.
Values may be sent and summed in bfloat16 or wider, within the bound.
A program may use at most 64 MiB of HBM per device.

v0:
```python
import jax
import jax.numpy as jnp
from jax import lax
from jax.sharding import PartitionSpec as P

CLASSES = 200
BASINS = 4


def bin_rows(transport, sigma_class, basin_id, depth_levels):
    depth_count, row_count, col_count = sigma_class.shape
    block_rows = 8
    block_count = row_count // block_rows
    cell_count = depth_count * col_count
    level_index = lax.broadcasted_iota(jnp.int32, (block_rows, depth_count, col_count), 1)
    class_iota = lax.broadcasted_iota(jnp.int32, (1, CLASSES, 1), 1)
    basin_iota = lax.broadcasted_iota(jnp.int32, (1, BASINS, 1), 1)

    def one_block(start):
        flow = jnp.transpose(lax.dynamic_slice_in_dim(transport, start, block_rows, 1), (1, 0, 2))
        klass = jnp.transpose(
            lax.dynamic_slice_in_dim(sigma_class, start, block_rows, 1), (1, 0, 2)
        )
        basin = lax.dynamic_slice_in_dim(basin_id, start, block_rows, 0)
        depth = lax.dynamic_slice_in_dim(depth_levels, start, block_rows, 0)
        wet_cells = level_index < depth[:, None, :]
        masked = jnp.where(wet_cells, flow, jnp.zeros_like(flow)).reshape(block_rows, 1, cell_count)
        basin_cells = jnp.broadcast_to(
            basin[:, None, :], (block_rows, depth_count, col_count)
        ).reshape(block_rows, 1, cell_count)
        basin_flow = jnp.where(basin_cells == basin_iota, masked, jnp.zeros_like(masked))
        class_hot = (klass.reshape(block_rows, 1, cell_count) == class_iota).astype(jnp.bfloat16)
        return jnp.einsum("rcn,rbn->rbc", class_hot, basin_flow, preferred_element_type=jnp.float32)

    starts = jnp.arange(block_count) * block_rows
    tables = lax.map(one_block, starts)
    return jnp.transpose(tables.reshape(row_count, BASINS, CLASSES), (1, 2, 0))


def body(transport, sigma_class, basin_id, depth_levels):
    table = bin_rows(transport, sigma_class, basin_id, depth_levels)
    shares = lax.psum_scatter(table, "lon", scatter_dimension=2, tiled=True)
    overturn = jnp.cumsum(shares, axis=1).astype(jnp.bfloat16)
    return lax.all_gather(overturn, ("lat", "lon"), axis=2, tiled=True)


def solution(mesh):
    placed = (P(None, "lat", "lon"), P(None, "lat", "lon"), P("lat", "lon"), P("lat", "lon"))
    return jax.shard_map(body, mesh=mesh, in_specs=placed, out_specs=P(), check_vma=False)
```

profile of v0, /device:TPU:0, one launch (start us, length us, event | category | flops | bytes accessed | tf_op | source)
XLA Modules:
  0.0 477.0 jit_solution(9716318747459529076)
XLA Ops:
  6.5 380.7 %while.11 = (s32[]{:T(128)}, f32[16,8,4,200]{3,2,1,0:T(4,128)S(1)}, s32[16]{0:T(128)S(1)}, s32[128,384]{1,0:T(8,128)}, s32[128,384]{1,0:T(8,128)}, /*index=5*/bf...) while((s32[]{:T(128)}, f32[16,8,4,200]{3,2,1,0:T(4,128)S(1)}, ...), condition=%wide.region_1.2_spmd.clone, body=%wide.region_0.1_spmd.clone.sunk | while | flops 266895360 | bytes 3940515 | solution.py:36
  9.3 0.8 constant_dynamic-slice_fusion.6
  10.1 1.2 fusion.29
  11.3 1.4 constant_dynamic-slice_fusion.5
  12.7 17.7 %fusion.30 = f32[16,8,4,200]{3,2,1,0:T(4,128)S(1)} fusion(f32[16,8,4,200]{3,2,1,0:T(4,128)S(1)} %get-tuple-element.150, s32[]{:T(128)} %get-tuple-element.149, s32[8,18432]{1,0:T(8,128)S(1)} %bitcast.46, s32[8,18432]{1,0:T(8,128)S(1)} %bitcast.45, bf16[8,18432]{1,0:T(8,128)(2,1)S(1)} %bitcast.47), kind=kOutput, calls=%fused_computation.10.clone.1 | convolution fusion | flops 266600448 | bytes 1507332 | tf_op jit(solution)/shard_map/while/body/eval_jaxpr/rcn,rbn->rbc/dot_general | solution.py:33
  33.1 0.8 constant_dynamic-slice_fusion.6
  33.9 1.2 fusion.29
  35.1 1.4 constant_dynamic-slice_fusion.5
  36.5 17.7 %fusion.30 = f32[16,8,4,200]{3,2,1,0:T(4,128)S(1)} fusion(f32[16,8,4,200]{3,2,1,0:T(4,128)S(1)} %get-tuple-element.150, s32[]{:T(128)} %get-tuple-element.149, s32[8,18432]{1,0:T(8,128)S(1)} %bitcast.46, s32[8,18432]{1,0:T(8,128)S(1)} %bitcast.45, bf16[8,18432]{1,0:T(8,128)(2,1)S(1)} %bitcast.47), kind=kOutput, calls=%fused_computation.10.clone.1 | convolution fusion | flops 266600448 | bytes 1507332 | tf_op jit(solution)/shard_map/while/body/eval_jaxpr/rcn,rbn->rbc/dot_general | solution.py:33
  56.9 0.8 constant_dynamic-slice_fusion.6
  57.7 1.2 fusion.29
  58.9 1.4 constant_dynamic-slice_fusion.5
  60.3 17.7 %fusion.30 = f32[16,8,4,200]{3,2,1,0:T(4,128)S(1)} fusion(f32[16,8,4,200]{3,2,1,0:T(4,128)S(1)} %get-tuple-element.150, s32[]{:T(128)} %get-tuple-element.149, s32[8,18432]{1,0:T(8,128)S(1)} %bitcast.46, s32[8,18432]{1,0:T(8,128)S(1)} %bitcast.45, bf16[8,18432]{1,0:T(8,128)(2,1)S(1)} %bitcast.47), kind=kOutput, calls=%fused_computation.10.clone.1 | convolution fusion | flops 266600448 | bytes 1507332 | tf_op jit(solution)/shard_map/while/body/eval_jaxpr/rcn,rbn->rbc/dot_general | solution.py:33
  80.7 0.8 constant_dynamic-slice_fusion.6
  81.5 1.2 fusion.29
  82.7 1.4 constant_dynamic-slice_fusion.5
  84.1 17.7 %fusion.30 = f32[16,8,4,200]{3,2,1,0:T(4,128)S(1)} fusion(f32[16,8,4,200]{3,2,1,0:T(4,128)S(1)} %get-tuple-element.150, s32[]{:T(128)} %get-tuple-element.149, s32[8,18432]{1,0:T(8,128)S(1)} %bitcast.46, s32[8,18432]{1,0:T(8,128)S(1)} %bitcast.45, bf16[8,18432]{1,0:T(8,128)(2,1)S(1)} %bitcast.47), kind=kOutput, calls=%fused_computation.10.clone.1 | convolution fusion | flops 266600448 | bytes 1507332 | tf_op jit(solution)/shard_map/while/body/eval_jaxpr/rcn,rbn->rbc/dot_general | solution.py:33
  105.3 1.2 fusion.29
  106.6 1.4 constant_dynamic-slice_fusion.5
  107.9 17.7 %fusion.30 = f32[16,8,4,200]{3,2,1,0:T(4,128)S(1)} fusion(f32[16,8,4,200]{3,2,1,0:T(4,128)S(1)} %get-tuple-element.150, s32[]{:T(128)} %get-tuple-element.149, s32[8,18432]{1,0:T(8,128)S(1)} %bitcast.46, s32[8,18432]{1,0:T(8,128)S(1)} %bitcast.45, bf16[8,18432]{1,0:T(8,128)(2,1)S(1)} %bitcast.47), kind=kOutput, calls=%fused_computation.10.clone.1 | convolution fusion | flops 266600448 | bytes 1507332 | tf_op jit(solution)/shard_map/while/body/eval_jaxpr/rcn,rbn->rbc/dot_general | solution.py:33
  128.4 0.8 constant_dynamic-slice_fusion.6
  129.1 1.2 fusion.29
  130.4 1.4 constant_dynamic-slice_fusion.5
  131.7 17.7 %fusion.30 = f32[16,8,4,200]{3,2,1,0:T(4,128)S(1)} fusion(f32[16,8,4,200]{3,2,1,0:T(4,128)S(1)} %get-tuple-element.150, s32[]{:T(128)} %get-tuple-element.149, s32[8,18432]{1,0:T(8,128)S(1)} %bitcast.46, s32[8,18432]{1,0:T(8,128)S(1)} %bitcast.45, bf16[8,18432]{1,0:T(8,128)(2,1)S(1)} %bitcast.47), kind=kOutput, calls=%fused_computation.10.clone.1 | convolution fusion | flops 266600448 | bytes 1507332 | tf_op jit(solution)/shard_map/while/body/eval_jaxpr/rcn,rbn->rbc/dot_general | solution.py:33
  152.2 0.8 constant_dynamic-slice_fusion.6
  152.9 1.2 fusion.29
  154.2 1.4 constant_dynamic-slice_fusion.5
  155.5 17.7 %fusion.30 = f32[16,8,4,200]{3,2,1,0:T(4,128)S(1)} fusion(f32[16,8,4,200]{3,2,1,0:T(4,128)S(1)} %get-tuple-element.150, s32[]{:T(128)} %get-tuple-element.149, s32[8,18432]{1,0:T(8,128)S(1)} %bitcast.46, s32[8,18432]{1,0:T(8,128)S(1)} %bitcast.45, bf16[8,18432]{1,0:T(8,128)(2,1)S(1)} %bitcast.47), kind=kOutput, calls=%fused_computation.10.clone.1 | convolution fusion | flops 266600448 | bytes 1507332 | tf_op jit(solution)/shard_map/while/body/eval_jaxpr/rcn,rbn->rbc/dot_general | solution.py:33
  176.0 0.8 constant_dynamic-slice_fusion.6
  176.8 1.2 fusion.29
  178.0 1.4 constant_dynamic-slice_fusion.5
  179.4 17.7 %fusion.30 = f32[16,8,4,200]{3,2,1,0:T(4,128)S(1)} fusion(f32[16,8,4,200]{3,2,1,0:T(4,128)S(1)} %get-tuple-element.150, s32[]{:T(128)} %get-tuple-element.149, s32[8,18432]{1,0:T(8,128)S(1)} %bitcast.46, s32[8,18432]{1,0:T(8,128)S(1)} %bitcast.45, bf16[8,18432]{1,0:T(8,128)(2,1)S(1)} %bitcast.47), kind=kOutput, calls=%fused_computation.10.clone.1 | convolution fusion | flops 266600448 | bytes 1507332 | tf_op jit(solution)/shard_map/while/body/eval_jaxpr/rcn,rbn->rbc/dot_general | solution.py:33
  199.8 0.8 constant_dynamic-slice_fusion.6
  200.6 1.2 fusion.29
  201.8 1.4 constant_dynamic-slice_fusion.5
  203.2 17.7 %fusion.30 = f32[16,8,4,200]{3,2,1,0:T(4,128)S(1)} fusion(f32[16,8,4,200]{3,2,1,0:T(4,128)S(1)} %get-tuple-element.150, s32[]{:T(128)} %get-tuple-element.149, s32[8,18432]{1,0:T(8,128)S(1)} %bitcast.46, s32[8,18432]{1,0:T(8,128)S(1)} %bitcast.45, bf16[8,18432]{1,0:T(8,128)(2,1)S(1)} %bitcast.47), kind=kOutput, calls=%fused_computation.10.clone.1 | convolution fusion | flops 266600448 | bytes 1507332 | tf_op jit(solution)/shard_map/while/body/eval_jaxpr/rcn,rbn->rbc/dot_general | solution.py:33
  223.6 0.8 constant_dynamic-slice_fusion.6
  224.4 1.2 fusion.29
  225.6 1.4 constant_dynamic-slice_fusion.5
  227.0 17.7 %fusion.30 = f32[16,8,4,200]{3,2,1,0:T(4,128)S(1)} fusion(f32[16,8,4,200]{3,2,1,0:T(4,128)S(1)} %get-tuple-element.150, s32[]{:T(128)} %get-tuple-element.149, s32[8,18432]{1,0:T(8,128)S(1)} %bitcast.46, s32[8,18432]{1,0:T(8,128)S(1)} %bitcast.45, bf16[8,18432]{1,0:T(8,128)(2,1)S(1)} %bitcast.47), kind=kOutput, calls=%fused_computation.10.clone.1 | convolution fusion | flops 266600448 | bytes 1507332 | tf_op jit(solution)/shard_map/while/body/eval_jaxpr/rcn,rbn->rbc/dot_general | solution.py:33
  248.2 1.2 fusion.29
  249.4 1.4 constant_dynamic-slice_fusion.5
  250.8 17.7 %fusion.30 = f32[16,8,4,200]{3,2,1,0:T(4,128)S(1)} fusion(f32[16,8,4,200]{3,2,1,0:T(4,128)S(1)} %get-tuple-element.150, s32[]{:T(128)} %get-tuple-element.149, s32[8,18432]{1,0:T(8,128)S(1)} %bitcast.46, s32[8,18432]{1,0:T(8,128)S(1)} %bitcast.45, bf16[8,18432]{1,0:T(8,128)(2,1)S(1)} %bitcast.47), kind=kOutput, calls=%fused_computation.10.clone.1 | convolution fusion | flops 266600448 | bytes 1507332 | tf_op jit(solution)/shard_map/while/body/eval_jaxpr/rcn,rbn->rbc/dot_general | solution.py:33
  272.0 1.2 fusion.29
  273.3 1.4 constant_dynamic-slice_fusion.5
  274.6 17.7 %fusion.30 = f32[16,8,4,200]{3,2,1,0:T(4,128)S(1)} fusion(f32[16,8,4,200]{3,2,1,0:T(4,128)S(1)} %get-tuple-element.150, s32[]{:T(128)} %get-tuple-element.149, s32[8,18432]{1,0:T(8,128)S(1)} %bitcast.46, s32[8,18432]{1,0:T(8,128)S(1)} %bitcast.45, bf16[8,18432]{1,0:T(8,128)(2,1)S(1)} %bitcast.47), kind=kOutput, calls=%fused_computation.10.clone.1 | convolution fusion | flops 266600448 | bytes 1507332 | tf_op jit(solution)/shard_map/while/body/eval_jaxpr/rcn,rbn->rbc/dot_general | solution.py:33
  295.8 1.2 fusion.29
  297.1 1.4 constant_dynamic-slice_fusion.5
  298.4 17.7 %fusion.30 = f32[16,8,4,200]{3,2,1,0:T(4,128)S(1)} fusion(f32[16,8,4,200]{3,2,1,0:T(4,128)S(1)} %get-tuple-element.150, s32[]{:T(128)} %get-tuple-element.149, s32[8,18432]{1,0:T(8,128)S(1)} %bitcast.46, s32[8,18432]{1,0:T(8,128)S(1)} %bitcast.45, bf16[8,18432]{1,0:T(8,128)(2,1)S(1)} %bitcast.47), kind=kOutput, calls=%fused_computation.10.clone.1 | convolution fusion | flops 266600448 | bytes 1507332 | tf_op jit(solution)/shard_map/while/body/eval_jaxpr/rcn,rbn->rbc/dot_general | solution.py:33
  319.6 1.2 fusion.29
  320.9 1.4 constant_dynamic-slice_fusion.5
  322.2 17.7 %fusion.30 = f32[16,8,4,200]{3,2,1,0:T(4,128)S(1)} fusion(f32[16,8,4,200]{3,2,1,0:T(4,128)S(1)} %get-tuple-element.150, s32[]{:T(128)} %get-tuple-element.149, s32[8,18432]{1,0:T(8,128)S(1)} %bitcast.46, s32[8,18432]{1,0:T(8,128)S(1)} %bitcast.45, bf16[8,18432]{1,0:T(8,128)(2,1)S(1)} %bitcast.47), kind=kOutput, calls=%fused_computation.10.clone.1 | convolution fusion | flops 266600448 | bytes 1507332 | tf_op jit(solution)/shard_map/while/body/eval_jaxpr/rcn,rbn->rbc/dot_general | solution.py:33
  343.5 1.2 fusion.29
  344.7 1.4 constant_dynamic-slice_fusion.5
  346.1 17.7 %fusion.30 = f32[16,8,4,200]{3,2,1,0:T(4,128)S(1)} fusion(f32[16,8,4,200]{3,2,1,0:T(4,128)S(1)} %get-tuple-element.150, s32[]{:T(128)} %get-tuple-element.149, s32[8,18432]{1,0:T(8,128)S(1)} %bitcast.46, s32[8,18432]{1,0:T(8,128)S(1)} %bitcast.45, bf16[8,18432]{1,0:T(8,128)(2,1)S(1)} %bitcast.47), kind=kOutput, calls=%fused_computation.10.clone.1 | convolution fusion | flops 266600448 | bytes 1507332 | tf_op jit(solution)/shard_map/while/body/eval_jaxpr/rcn,rbn->rbc/dot_general | solution.py:33
  367.2 1.1 fusion.29
  368.4 1.1 constant_dynamic-slice_fusion.5
  369.5 17.7 %fusion.30 = f32[16,8,4,200]{3,2,1,0:T(4,128)S(1)} fusion(f32[16,8,4,200]{3,2,1,0:T(4,128)S(1)} %get-tuple-element.150, s32[]{:T(128)} %get-tuple-element.149, s32[8,18432]{1,0:T(8,128)S(1)} %bitcast.46, s32[8,18432]{1,0:T(8,128)S(1)} %bitcast.45, bf16[8,18432]{1,0:T(8,128)(2,1)S(1)} %bitcast.47), kind=kOutput, calls=%fused_computation.10.clone.1 | convolution fusion | flops 266600448 | bytes 1507332 | tf_op jit(solution)/shard_map/while/body/eval_jaxpr/rcn,rbn->rbc/dot_general | solution.py:33
  387.2 0.9 copy.18
  388.1 34.0 %reduce-scatter.2.cloned.1.call-done = f32[4,200,16]{1,2,0:T(8,128)} async-done(((f32[4,200,128]{1,2,0:T(8,128)}), f32[4,200,16]{1,2,0:T(8,128)}) %reduce-scatter.2.cloned.1.call-update) | async-done | bytes 51216 | tf_op jit(solution)/shard_map/reduce_scatter | solution.py:42
  422.2 0.8 copy_bitcast_fusion.1
  423.0 2.3 reduce-window.6
  425.6 43.3 %all_gather.3 = bf16[4,200,512]{1,2,0:T(8,128)(2,1)S(1)} all-gather(bf16[4,200,16]{1,2,0:T(8,128)(2,1)S(1)} %bitcast.50), channel_id=1, replica_groups=mesh['lat'=4,'lon'=8] {'lat','lon'}, dimensions={2}, use_global_device_ids=true | all-gather | bytes 844800 | tf_op jit(solution)/shard_map/all_gather | solution.py:44
  468.9 1.2 copy.12
  (49 shorter events, 17.0 us)
Async XLA Ops:
  6.5 415.6 %reduce-scatter.2.cloned.1.call-start = ((), (), s32[]{:S(2)}) async-start(), calls=%async_computation.1 | async-start | bytes 589824 | tf_op jit(solution)/shard_map/reduce_scatter | solution.py:42
Sparse Core Ops, SparseCore 0:
  388.3 33.8 reduce-scatter.1
where the time goes:
time: 480 us; the launch traced here: 477 us
  matrix products  283 us (59%)
  local copies, waits for them, and re-layouts  48.3 us (10%)
  blocking collectives  43.3 us (9%)
  waiting for transfers between devices  34 us (7%)
  loops' own time  33.4 us (7%)
  other arithmetic  21.5 us (4%)
  between operations  13.4 us (3%)
    dot_general x16, matrix products, one_block(): jnp.einsum('rcn,rbn->rbc', class_hot, basin_flow, preferred_element_type=...  283 us
    all_gather x1, blocking collectives, body(): return lax.all_gather(overturn, ('lat', 'lon'), axis=2, tiled=True)  43.3 us
    reduce_scatter x1, waiting for transfers between devices, body(): shares = lax.psum_scatter(table, 'lon', scatter_dimension=2, tiled=True)  34 us
    another operation x1, loops' own time, bin_rows(): tables = lax.map(one_block, starts)  33.4 us
    dynamic_slice x16, local copies, waits for them, and re-layouts, one_block(): lax.dynamic_slice_in_dim(sigma_class, start, block_rows, 1)  21.4 us
    select_n x16, other arithmetic, one_block(): jnp.where(wet_cells, flow, jnp.zeros_like(flow))  19.1 us
    dynamic_slice x16, local copies, waits for them, and re-layouts, one_block(): depth = lax.dynamic_slice_in_dim(depth_levels, start, block_rows, 0)  12.3 us
    dynamic_slice x16, local copies, waits for them, and re-layouts, bin_rows(): tables = lax.map(one_block, starts)  10.7 us
  transfers between devices with their start and end apart: 1, of which 1 were waited for; matrix products, arithmetic and copies ran while one was open for 0% of the time, Pallas kernels for 0%

commit v1 on v0

v1 whole, which is shorter than its diff:
```python
import functools

import jax
import jax.numpy as jnp
import numpy as np
from jax import lax
from jax.experimental import pallas as pl
from jax.experimental.pallas import tpu as pltpu
from jax.sharding import PartitionSpec as P

CLASSES = 200
BASINS = 4
SUB = 8
LANES = 128
TILE = 256
STEP_ROWS = 16
MESH = pl.DeviceIdType.MESH
HIGHS = 26
HIGH_BLOCKS = 4


def hot_pairs(index, count, value):
    return [jnp.where(index == jnp.bfloat16(2 * i), value, jnp.bfloat16(0)) for i in range(count)]


def doubled(index):
    pair = jnp.concatenate([index, index - 1], axis=0)
    return pair.astype(jnp.float32).astype(jnp.bfloat16)


def squeeze_rows(product):
    rows = lax.broadcasted_iota(jnp.int32, (SUB, TILE), 0)
    lanes = lax.broadcasted_iota(jnp.int32, (SUB, TILE), 1)
    own = (lanes % SUB) == rows
    blocks = []
    for q in range(HIGH_BLOCKS):
        total = None
        for s in range(SUB):
            high = q * SUB + s
            if high * SUB >= CLASSES:
                break
            piece = jnp.where(own, product[high * SUB:(high + 1) * SUB, :], 0.0)
            piece = piece if s == 0 else pltpu.roll(piece, s, 1)
            total = piece if total is None else total + piece
        straight = jnp.where(rows == 0, total, 0.0)
        for r in range(1, SUB):
            straight = jnp.where(rows == r, pltpu.roll(total, TILE - r, 1), straight)
        blocks.append(straight)
    return jnp.concatenate(blocks, axis=1)


def bin_kernel(flow_ref, class_ref, basin_ref, depth_ref, out_ref, acc_ref):
    levels, _, cols = class_ref.shape
    chunks = cols // LANES
    per_trip = 4
    for half in range(STEP_ROWS // SUB):
        rows = slice(half * SUB, (half + 1) * SUB)

        def trip(t, carry, rows=rows):
            tiles = []
            for u in range(per_trip):
                level = t * per_trip + u
                for c in range(chunks):
                    lanes = slice(c * LANES, (c + 1) * LANES)
                    klass = class_ref[level, rows, lanes]
                    flow = flow_ref[level, :, lanes].astype(jnp.float32)[rows]
                    flow = jnp.where(level < depth_ref[rows, lanes], flow, 0.0)
                    high = doubled(klass >> 3)
                    low = doubled(basin_ref[rows, lanes] * SUB + (klass & 7))
                    value = jnp.concatenate([flow, flow], axis=0).astype(jnp.bfloat16)
                    tiles.append((
                        jnp.concatenate(hot_pairs(high, HIGHS // 2, value), axis=0),
                        jnp.concatenate(hot_pairs(low, TILE // (2 * SUB), jnp.bfloat16(1)), axis=0),
                    ))
            left = jnp.concatenate([x for x, _ in tiles], axis=1)
            right = jnp.concatenate([y for _, y in tiles], axis=1)
            acc_ref[...] += lax.dot_general(
                left, right, (((1,), (1,)), ((), ())), preferred_element_type=jnp.float32
            )
            return carry

        acc_ref[...] = jnp.zeros_like(acc_ref)
        lax.fori_loop(0, levels // per_trip, trip, 0)
        product = acc_ref[...]
        out_ref[rows, :] = squeeze_rows(product)


def bin_rows(transport, sigma_class, basin_id, depth_levels):
    levels, row_count, cols = sigma_class.shape
    deep = pl.BlockSpec((levels, STEP_ROWS, cols), lambda i: (0, i, 0))
    flat = pl.BlockSpec((STEP_ROWS, cols), lambda i: (i, 0))
    width = HIGH_BLOCKS * TILE
    return pl.pallas_call(
        bin_kernel,
        grid=(row_count // STEP_ROWS,),
        in_specs=[deep, deep, flat, flat],
        out_specs=pl.BlockSpec((STEP_ROWS, width), lambda i: (i, 0)),
        out_shape=jax.ShapeDtypeStruct((row_count, width), jnp.float32),
        scratch_shapes=[pltpu.VMEM((HIGHS * SUB, TILE), jnp.float32)],
        name="bin_rows",
    )(transport, sigma_class, basin_id, depth_levels)


def running_sums():
    row = np.arange(HIGH_BLOCKS * LANES)
    column = np.arange(2 * TILE)
    lane = row % LANES
    klass = (row // LANES) * 64 + (lane % SUB) * SUB + (lane % 64) // SUB
    same = (lane // 64)[:, None] == (column // TILE)[None, :]
    return (same & (klass[:, None] <= (column % TILE)[None, :])).astype(jnp.bfloat16)


def accumulate(share, sums):
    pieces = []
    for pair in range(BASINS // 2):
        lanes = [share[:, q * TILE + pair * LANES:q * TILE + (pair + 1) * LANES] for q in range(HIGH_BLOCKS)]
        rest = jnp.concatenate(lanes, axis=1)
        total = None
        for _ in range(3):
            part = rest.astype(jnp.bfloat16)
            rest = rest - part.astype(jnp.float32)
            term = jnp.dot(part, sums, preferred_element_type=jnp.float32)
            total = term if total is None else total + term
        pieces.append(total)
    return jnp.concatenate(pieces, axis=1)


def share_kernel(lats, lons, table_ref, sums_ref, out_ref, half, acc, arrived, sums, sum_sem,
                 half_send, half_recv, arr_send, arr_recv, out_send, out_recv):
    lat, lon = lax.axis_index("lat"), lax.axis_index("lon")
    zs = lons // 2
    z, core = lon // 2, lax.rem(lon, 2)
    partner = (lat, z * 2 + (1 - core))
    z_peers = [(lat, lax.rem(z + k, zs) * 2 + core) for k in range(1, zs)]
    lat_peers = [(lax.rem(lat + k, lats), lon) for k in range(1, lats)]

    load = pltpu.make_async_copy(sums_ref, sums, sum_sem)
    load.start()
    barrier = pltpu.get_barrier_semaphore()
    everyone = [partner] + z_peers + lat_peers
    for peer in everyone:
        pl.semaphore_signal(barrier, inc=1, device_id=peer, device_id_type=MESH)
    pl.semaphore_wait(barrier, len(everyone))

    def send(src, dst, send_sem, recv_sem, peer):
        copy = pltpu.make_async_remote_copy(
            src_ref=src, dst_ref=dst, send_sem=send_sem, recv_sem=recv_sem,
            device_id=peer, device_id_type=MESH,
        )
        copy.start()
        return copy

    swaps = []
    for k in [*range(1, zs), 0]:
        d = lax.rem(z + k, zs)
        swaps.append((k, send(table_ref.at[2 * d + (1 - core)], half.at[k], half_send.at[k], half_recv.at[k], partner)))
    moves = []
    for k, swap in swaps:
        swap.wait_recv()
        d = lax.rem(z + k, zs)
        acc[k] = table_ref[2 * d + core] + half[k]
        if k > 0:
            moves.append(send(acc.at[k], arrived.at[k - 1], arr_send.at[k - 1], arr_recv.at[k - 1], z_peers[k - 1]))
    share = acc[0]
    for k in range(1, zs):
        moves[k - 1].wait_recv()
        share = share + arrived[k - 1]
    load.wait()
    me = lat * lons + lon
    out_ref[me] = accumulate(share, sums[...]).astype(jnp.bfloat16)

    copies = []

    def spread(owner, peer):
        n = len(copies)
        copies.append(send(out_ref.at[owner], out_ref.at[owner], out_send.at[n], out_recv.at[owner], peer))

    def landed(owner):
        pltpu.make_async_remote_copy(
            src_ref=out_ref.at[owner], dst_ref=out_ref.at[owner], send_sem=out_send.at[0],
            recv_sem=out_recv.at[owner], device_id=partner, device_id_type=MESH,
        ).wait_recv()

    for peer in z_peers + lat_peers:
        spread(me, peer)
    spread(me, partner)
    for k in range(1, zs):
        owner = lat * lons + lax.rem(z - k + zs, zs) * 2 + core
        landed(owner)
        for peer in lat_peers + [partner]:
            spread(owner, peer)
    for j in range(zs):
        for k in range(1, lats):
            owner = lax.rem(lat - k + lats, lats) * lons + lax.rem(z - j + zs, zs) * 2 + core
            landed(owner)
            spread(owner, partner)
    for j in range(zs):
        for k in range(lats):
            landed(lax.rem(lat - k + lats, lats) * lons + lax.rem(z - j + zs, zs) * 2 + (1 - core))
    for _, swap in swaps:
        swap.wait_send()
    for move in moves:
        move.wait_send()
    for copy in copies:
        copy.wait_send()


def share_rows(lats, lons, table):
    rows = table.shape[0] // lons
    width = table.shape[1]
    zs = lons // 2
    sends = (zs - 1) + (lats - 1) + 1 + (zs - 1) * lats + zs * (lats - 1)
    dma = pltpu.SemaphoreType.DMA
    return pl.pallas_call(
        functools.partial(share_kernel, lats, lons),
        out_shape=jax.ShapeDtypeStruct((lats * lons, rows, width), jnp.bfloat16),
        in_specs=[pl.BlockSpec(memory_space=pltpu.VMEM), pl.BlockSpec(memory_space=pl.ANY)],
        out_specs=pl.BlockSpec(memory_space=pltpu.VMEM),
        scratch_shapes=[
            pltpu.VMEM((zs, rows, width), jnp.float32),
            pltpu.VMEM((zs, rows, width), jnp.float32),
            pltpu.VMEM((zs - 1, rows, width), jnp.float32),
            pltpu.VMEM((HIGH_BLOCKS * LANES, 2 * TILE), jnp.bfloat16),
            dma(()),
            dma((zs,)), dma((zs,)), dma((zs - 1,)), dma((zs - 1,)),
            dma((sends,)), dma((lats * lons,)),
        ],
        compiler_params=pltpu.CompilerParams(collective_id=0, has_side_effects=True),
        name="share_rows",
    )(table.reshape(lons, rows, width), jnp.asarray(running_sums()))


def body(lats, lons, transport, sigma_class, basin_id, depth_levels):
    table = bin_rows(transport, sigma_class, basin_id, depth_levels)
    whole = share_rows(lats, lons, table).reshape(-1, BASINS, TILE)
    return jnp.transpose(whole[:, :, :CLASSES], (1, 2, 0))


def solution(mesh):
    placed = (P(None, "lat", "lon"), P(None, "lat", "lon"), P("lat", "lon"), P("lat", "lon"))
    local = functools.partial(body, mesh.shape["lat"], mesh.shape["lon"])
    return jax.shard_map(local, mesh=mesh, in_specs=placed, out_specs=P(), check_vma=False)
```

time: 480 us -> 118 us (0.25)
  matrix products: 283 us -> 0 us
  Pallas kernels: 0 us -> 114 us
  local copies, waits for them, and re-layouts: 48.3 us -> 3.27 us
  blocking collectives: 43.3 us -> 0 us
  waiting for transfers between devices: 34 us -> 0 us
  loops' own time: 33.4 us -> 0 us
  other arithmetic: 21.5 us -> 0 us
  between operations: 13.4 us -> 0.02 us
    dot_general x16 -> x0, matrix products: 283 us -> none  [one_block(): jnp.einsum('rcn,rbn->rbc', class_hot, basin_flow, preferred_element_type=...]
    pallas_call x0 -> x2, Pallas kernels: none -> 114 us  [the longest x1 86.7 us: bin_rows(): pl.pallas_call(bin_kernel, grid=(row_count // STEP_ROWS,), in_specs=[deep...]
    dynamic_slice x48 -> x0, local copies, waits for them, and re-layouts: 44.4 us -> none  [the longest x16 21.4 us: one_block(): lax.dynamic_slice_in_dim(sigma_class, start, block_rows, 1)]
    all_gather x1 -> x0, blocking collectives: 43.3 us -> none  [body(): return lax.all_gather(overturn, ('lat', 'lon'), axis=2, tiled=True)]
    reduce_scatter x1 -> x0, waiting for transfers between devices: 34 us -> none  [body(): shares = lax.psum_scatter(table, 'lon', scatter_dimension=2, tiled=True)]
    another operation x1 -> x0, loops' own time: 33.4 us -> none  [bin_rows(): tables = lax.map(one_block, starts)]
    select_n x16 -> x0, other arithmetic: 19.1 us -> none  [one_block(): jnp.where(wet_cells, flow, jnp.zeros_like(flow))]
  transfers between devices with their start and end apart: 1 -> 0, of which waited for: 1 -> 0; matrix products, arithmetic and copies ran while one was open for 0% -> 0% of each run, Pallas kernels for 0% -> 0%
where the time goes in v1:
time: 118 us
  Pallas kernels  114 us (97%)
  local copies, waits for them, and re-layouts  3.27 us (3%)
    pallas_call x1, Pallas kernels, bin_rows(): pl.pallas_call(bin_kernel, grid=(row_count // STEP_ROWS,), in_specs=[deep...  86.7 us
    pallas_call x1, Pallas kernels, share_rows(): pl.pallas_call(functools.partial(share_kernel, lats, lons), out_shape=jax...  27.7 us

profile of v1, /device:TPU:0, one launch (start us, length us, event | category | flops | bytes accessed | tf_op | source)
XLA Modules:
  0.0 117.6 jit_solution(9496480520317575426)
XLA Ops:
  0.0 86.7 %bin_rows.1 = f32[128,1024]{1,0:T(8,128)} custom-call(bf16[48,128,384]{2,1,0:T(8,128)(2,1)} %flow_ref.1, s32[48,128,384]{2,1,0:T(8,128)} %class_ref.1, s32[128,384]{1,0:T(8,128)} %basin_ref.1, s32[128,384]{1,0:T(8,128)} %depth_ref.1), custom_call_target="tpu_custom_call" | custom-call | tf_op jit(solution)/shard_map/bin_rows/pallas_call | solution.py:93
  86.7 27.7 %share_rows.1 = bf16[32,16,1024]{2,1,0:T(8,128)(2,1)} custom-call(f32[8,16,1024]{2,1,0:T(8,128)} %bitcast.4, bf16[512,512]{1,0:T(8,128)(2,1)} %constant.2.clone.sums_ref), custom_call_target="tpu_custom_call" | custom-call | tf_op jit(solution)/shard_map/share_rows/pallas_call | solution.py:214
  114.3 1.9 %reshape.7 = bf16[512,4,256]{2,1,0:T(4,128)(2,1)S(1)} reshape(bf16[32,16,1024]{2,1,0:T(8,128)(2,1)} %share_rows.1) | data formatting | bytes 2097152 | tf_op jit(solution)/shard_map/reshape | solution.py:235
  116.2 1.4 %copy.7 = bf16[512,4,200]{0,2,1:T(8,128)(2,1)} copy(bf16[512,4,200]{2,1,0:T(4,128)(2,1)S(1)} %bitcast.3) | data formatting | bytes 1638400

commit v2 on v1

--- a/solution.py
+++ b/solution.py
@@ -49,10 +49,10 @@
     return jnp.concatenate(blocks, axis=1)
 
 
-def bin_kernel(flow_ref, class_ref, basin_ref, depth_ref, out_ref, acc_ref):
+def bin_block(flow_ref, class_ref, basin_ref, depth_ref, out_ref, *accs):
     levels, _, cols = class_ref.shape
     chunks = cols // LANES
-    per_trip = 4
+    per_trip = 16
     for half in range(STEP_ROWS // SUB):
         rows = slice(half * SUB, (half + 1) * SUB)
 
@@ -72,17 +72,24 @@
                         jnp.concatenate(hot_pairs(high, HIGHS // 2, value), axis=0),
                         jnp.concatenate(hot_pairs(low, TILE // (2 * SUB), jnp.bfloat16(1)), axis=0),
                     ))
-            left = jnp.concatenate([x for x, _ in tiles], axis=1)
-            right = jnp.concatenate([y for _, y in tiles], axis=1)
-            acc_ref[...] += lax.dot_general(
-                left, right, (((1,), (1,)), ((), ())), preferred_element_type=jnp.float32
-            )
+            for k in range(0, len(tiles), 2):
+                mxu, stage = (k // 2) % 2, (k // 4) % 2
+                left = jnp.concatenate([tiles[k][0], tiles[k + 1][0]], axis=1)
+                right = jnp.concatenate([tiles[k][1], tiles[k + 1][1]], axis=1)
+                pltpu.matmul_push_rhs(right, staging_register=stage, mxu_index=mxu, transpose=True)
+                pltpu.matmul_acc_lhs(accs[mxu], left, load_staged_rhs=stage)
             return carry
 
-        acc_ref[...] = jnp.zeros_like(acc_ref)
         lax.fori_loop(0, levels // per_trip, trip, 0)
-        product = acc_ref[...]
+        product = pltpu.matmul_pop(accs[0]) + pltpu.matmul_pop(accs[1])
         out_ref[rows, :] = squeeze_rows(product)
+
+
+def bin_kernel(*refs):
+    shape = (HIGHS * SUB, TILE)
+    pl.run_scoped(
+        functools.partial(bin_block, *refs), *[pltpu.ACC(m)(shape, jnp.float32) for m in (0, 1)]
+    )
 
 
 def bin_rows(transport, sigma_class, basin_id, depth_levels):
@@ -96,7 +103,6 @@
         in_specs=[deep, deep, flat, flat],
         out_specs=pl.BlockSpec((STEP_ROWS, width), lambda i: (i, 0)),
         out_shape=jax.ShapeDtypeStruct((row_count, width), jnp.float32),
-        scratch_shapes=[pltpu.VMEM((HIGHS * SUB, TILE), jnp.float32)],
         name="bin_rows",
     )(transport, sigma_class, basin_id, depth_levels)
 

time: 118 us -> 87.5 us (0.74)
  Pallas kernels: 114 us -> 84 us
    pallas_call x1, Pallas kernels: 86.7 us -> 56.3 us  [bin_rows(): pl.pallas_call(bin_kernel, grid=(row_count // STEP_ROWS,), in_specs=[deep...]
where the time goes in v2:
time: 87.5 us; the launch traced here: 87.3 us
  Pallas kernels  84 us (96%)
  local copies, waits for them, and re-layouts  3.27 us (4%)
    pallas_call x1, Pallas kernels, bin_rows(): pl.pallas_call(bin_kernel, grid=(row_count // STEP_ROWS,), in_specs=[deep...  56.3 us
    pallas_call x1, Pallas kernels, share_rows(): pl.pallas_call(functools.partial(share_kernel, lats, lons), out_shape=jax...  27.7 us
    reshape x1, local copies, waits for them, and re-layouts, body(): whole = share_rows(lats, lons, table).reshape(-1, BASINS, TILE)  1.86 us

profile of v2, /device:TPU:0, one launch (start us, length us, event | category | flops | bytes accessed | tf_op | source)
XLA Modules:
  0.0 87.3 jit_solution(12476524629864961996)
XLA Ops:
  0.0 56.3 %bin_rows.1 = f32[128,1024]{1,0:T(8,128)} custom-call(bf16[48,128,384]{2,1,0:T(8,128)(2,1)} %refs_0_.1, s32[48,128,384]{2,1,0:T(8,128)} %refs_1_.1, s32[128,384]{1,0:T(8,128)} %refs_2_.1, s32[128,384]{1,0:T(8,128)} %refs_3_.1), custom_call_target="tpu_custom_call" | custom-call | tf_op jit(solution)/shard_map/bin_rows/pallas_call | solution.py:100
  56.3 27.7 %share_rows.1 = bf16[32,16,1024]{2,1,0:T(8,128)(2,1)} custom-call(f32[8,16,1024]{2,1,0:T(8,128)} %bitcast.4, bf16[512,512]{1,0:T(8,128)(2,1)} %constant.2.clone.sums_ref), custom_call_target="tpu_custom_call" | custom-call | tf_op jit(solution)/shard_map/share_rows/pallas_call | solution.py:220
  84.0 1.9 %reshape.7 = bf16[512,4,256]{2,1,0:T(4,128)(2,1)S(1)} reshape(bf16[32,16,1024]{2,1,0:T(8,128)(2,1)} %share_rows.1) | data formatting | bytes 2097152 | tf_op jit(solution)/shard_map/reshape | solution.py:241
  85.9 1.4 %copy.7 = bf16[512,4,200]{0,2,1:T(8,128)(2,1)} copy(bf16[512,4,200]{2,1,0:T(4,128)(2,1)S(1)} %bitcast.3) | data formatting | bytes 1638400

commit v3 on v2

--- a/solution.py
+++ b/solution.py
@@ -52,7 +52,7 @@
 def bin_block(flow_ref, class_ref, basin_ref, depth_ref, out_ref, *accs):
     levels, _, cols = class_ref.shape
     chunks = cols // LANES
-    per_trip = 16
+    per_trip = 24
     for half in range(STEP_ROWS // SUB):
         rows = slice(half * SUB, (half + 1) * SUB)
 

time: 87.5 us -> 86.3 us (0.986)
  Pallas kernels: 84 us -> 82.8 us
    pallas_call x1, Pallas kernels: 56.3 us -> 55.1 us  [bin_rows(): pl.pallas_call(bin_kernel, grid=(row_count // STEP_ROWS,), in_specs=[deep...]
where the time goes in v3:
time: 86.3 us; the launch traced here: 86.1 us
  Pallas kernels  82.8 us (96%)
  local copies, waits for them, and re-layouts  3.27 us (4%)
    pallas_call x1, Pallas kernels, bin_rows(): pl.pallas_call(bin_kernel, grid=(row_count // STEP_ROWS,), in_specs=[deep...  55.1 us
    pallas_call x1, Pallas kernels, share_rows(): pl.pallas_call(functools.partial(share_kernel, lats, lons), out_shape=jax...  27.7 us
    reshape x1, local copies, waits for them, and re-layouts, body(): whole = share_rows(lats, lons, table).reshape(-1, BASINS, TILE)  1.86 us

profile of v3, /device:TPU:0, one launch (start us, length us, event | category | flops | bytes accessed | tf_op | source)
XLA Modules:
  0.0 86.1 jit_solution(6979963579146115431)
XLA Ops:
  0.0 55.1 %bin_rows.1 = f32[128,1024]{1,0:T(8,128)} custom-call(bf16[48,128,384]{2,1,0:T(8,128)(2,1)} %refs_0_.1, s32[48,128,384]{2,1,0:T(8,128)} %refs_1_.1, s32[128,384]{1,0:T(8,128)} %refs_2_.1, s32[128,384]{1,0:T(8,128)} %refs_3_.1), custom_call_target="tpu_custom_call" | custom-call | tf_op jit(solution)/shard_map/bin_rows/pallas_call | solution.py:100
  55.1 27.7 %share_rows.1 = bf16[32,16,1024]{2,1,0:T(8,128)(2,1)} custom-call(f32[8,16,1024]{2,1,0:T(8,128)} %bitcast.4, bf16[512,512]{1,0:T(8,128)(2,1)} %constant.2.clone.sums_ref), custom_call_target="tpu_custom_call" | custom-call | tf_op jit(solution)/shard_map/share_rows/pallas_call | solution.py:220
  82.8 1.9 %reshape.7 = bf16[512,4,256]{2,1,0:T(4,128)(2,1)S(1)} reshape(bf16[32,16,1024]{2,1,0:T(8,128)(2,1)} %share_rows.1) | data formatting | bytes 2097152 | tf_op jit(solution)/shard_map/reshape | solution.py:241
  84.7 1.4 %copy.7 = bf16[512,4,200]{0,2,1:T(8,128)(2,1)} copy(bf16[512,4,200]{2,1,0:T(4,128)(2,1)S(1)} %bitcast.3) | data formatting | bytes 1638400
